TPU v7x, 128 devices: a whole 4x4x4 slice. The times are simulated.
128 devices in a mesh: row: 16 (over z, x_lo, core), col: 8 (over y, x_hi).
Axes of the slice: x: 4 (x_hi: 2, x_lo: 2; x = x_hi * 2 + x_lo), y: 4, z: 4, core: 2. Of those that a mesh axis runs over, the one named last changes fastest.
Arguments:
- loadings: bfloat16 [8, 32768, 1024], P(None, 'row', 'col'), may hold values from -6 to 6
- weights: bfloat16 [8, 32768, 512], P(None, 'row', 'col'), may hold values from -0.03125 to 0.03125
- specific: float32 [8, 32768], P(None, 'row'), may hold values from 0.2 to 5
- factor_cov: float32 [8, 1024, 1024], P(None, 'col'), may hold values from -0.001953125 to 0.0048828125, as said below
Outputs:
- portfolio_cov: float32 [8, 512, 512], P(None, 'row', 'col')
Inputs may be any that keep to these rules, and one draw needn't show every extreme that they name: `factor_cov`: each day's matrix is a symmetric positive definite factor covariance of order 1024.
All inputs are finite; a program needn't handle non-finite values.
Results may differ from a plain program's by a relative error of at most 0.0003.
Values may be sent and summed in bfloat16 or wider, within the bound.
A program may use at most 128 MiB of HBM per device.

v0:
```python
import jax
import jax.numpy as jnp
from jax import lax
from jax.sharding import PartitionSpec as P


def rows_for(lines, devices):
    spare = -len(lines) % devices
    return jnp.pad(lines, [(0, spare)] + [(0, 0)] * (lines.ndim - 1))


def sum_by_parts(value, axis):
    lines = value.reshape(-1, *value.shape[1:][-1:])
    padded = rows_for(lines, lax.axis_size(axis))
    own = lax.psum_scatter(padded, axis, scatter_dimension=0, tiled=True)
    whole = lax.all_gather(own, axis, axis=0, tiled=True)
    return whole[: len(lines)].reshape(value.shape)


def shards(loadings, weights, specific, factor_cov):
    factor_cols = loadings.shape[2]
    port_cols = weights.shape[2]
    total_ports = port_cols * lax.axis_size("col")
    port_rows = total_ports // lax.axis_size("row")
    row_start = lax.axis_index("row") * port_rows
    weighted = (specific[:, :, None] * weights.astype(jnp.float32)).astype(jnp.bfloat16)
    fragment = lax.all_gather(weights, "col", axis=2, tiled=True)
    exposure_part = jnp.einsum(
        "dar,dap->drp", loadings, fragment, preferred_element_type=jnp.float32
    )
    specific_term = jnp.einsum(
        "dak,dap->dkp", weighted, fragment, preferred_element_type=jnp.float32
    )
    joined = jnp.concatenate([exposure_part, specific_term], axis=1)
    totals = sum_by_parts(joined, "row")
    exposure = totals[:, :factor_cols, :]
    specific_block = lax.dynamic_slice_in_dim(totals[:, factor_cols:, :], row_start, port_rows, 2)
    exposure_rows = lax.dynamic_slice_in_dim(exposure, row_start, port_rows, 2)
    left_part = jnp.einsum(
        "dri,drs->dis", exposure_rows, factor_cov, precision=lax.Precision.HIGHEST
    )
    left = lax.psum(left_part, "col")
    exposure_cols = lax.all_to_all(exposure, "col", split_axis=2, concat_axis=1, tiled=True)
    factor_block = jnp.einsum("dir,drk->dik", left, exposure_cols, precision=lax.Precision.HIGHEST)
    return factor_block + jnp.swapaxes(specific_block, 1, 2)


def solution(mesh):
    in_specs = (P(None, "row", "col"), P(None, "row", "col"), P(None, "row"), P(None, "col", None))
    out_specs = P(None, "row", "col")
    return jax.shard_map(shards, mesh=mesh, in_specs=in_specs, out_specs=out_specs, check_vma=False)
```

profile of v0, /device:TPU:1, one launch (start us, length us, event | category | flops | bytes accessed | tf_op | source)
XLA Modules:
  0.0 437.0 jit_solution(14790586214625293099)
XLA Ops:
  6.5 0.0 copy-start
  6.5 0.0 all-gather.3.cloned.1.call-start
  6.5 0.7 all-gather.3.cloned.1.call-update
  7.3 0.0 reduce-scatter.2.cloned.1.call-start
  7.3 187.0 %all-gather.3.cloned.1.call-done = bf16[8,2048,512]{1,2,0:T(8,128)(2,1)} async-done(((bf16[8,2048,64]{1,2,0:T(8,128)(2,1)}), bf16[8,2048,512]{1,2,0:T(8,128)(2,1)}) %all-gather.3.cloned.1.call-update) | async-done | bytes 16777232 | tf_op jit(solution)/shard_map/all_gather | solution.py:27
  194.3 0.0 copy-done
  194.3 11.0 %fusion = f32[8,64,512]{2,1,0:T(8,128)S(1)} fusion(bf16[8,2048,512]{1,2,0:T(8,128)(2,1)} %all-gather.3.cloned.1.call-done, bf16[8,2048,64]{1,2,0:T(8,128)(2,1)S(1)} %copy-done, f32[8,2048]{1,0:T(8,128)} %param.6), kind=kOutput, calls=%fused_computation.2 | convolution fusion | flops 1076887552 | bytes 19988480 | tf_op jit(solution)/shard_map/dak,dap->dkp/dot_general | solution.py:31
  205.3 10.4 %fusion.5 = f32[8,128,512]{2,1,0:T(8,128)S(1)} fusion(bf16[8,2048,128]{2,1,0:T(8,128)(2,1)} %param.4, bf16[8,2048,512]{1,2,0:T(8,128)(2,1)} %all-gather.3.cloned.1.call-done), kind=kOutput, calls=%fused_computation.9 | convolution fusion | flops 2147483648 | bytes 23068672 | tf_op jit(solution)/shard_map/dar,dap->drp/dot_general | solution.py:28
  215.7 2.2 pad_maximum_fusion
  217.8 0.0 reduce-scatter.2.cloned.1.call-update
  217.9 0.0 all-gather.5.cloned.1.call-start
  217.9 63.7 %reduce-scatter.2.cloned.1.call-done = f32[96,512]{1,0:T(8,128)} async-done(((f32[1536,512]{1,0:T(8,128)}), f32[96,512]{1,0:T(8,128)}) %reduce-scatter.2.cloned.1.call-update) | async-done | bytes 196624 | tf_op jit(solution)/shard_map/reduce_scatter | solution.py:15
  281.6 0.0 all-gather.5.cloned.1.call-update
  281.6 38.9 %all-gather.5.cloned.1.call-done = f32[1536,512]{1,0:T(8,128)} async-done(((f32[96,512]{1,0:T(8,128)}), f32[1536,512]{1,0:T(8,128)}) %all-gather.5.cloned.1.call-update) | async-done | bytes 3145744 | tf_op jit(solution)/shard_map/all_gather | solution.py:16
  320.6 1.9 slice.8
  322.4 1.8 copy.16
  324.3 6.2 %all-to-all-start = ((f32[8,128,512]{1,0,2:T(8,128)}), f32[8,128,512]{1,0,2:T(8,128)}, u32[]{:S(2)}, u32[]{:S(2)}) async-start(f32[8,128,512]{1,0,2:T(8,128)} %copy.16), calls=%async_computation.1 | async-start | bytes 4194304 | tf_op jit(solution)/shard_map/all_to_all | solution.py:43
  330.5 0.2 all-reduce.2.cloned.1.call-start
  330.7 5.7 %fusion.2 = f32[8,32,1024]{2,1,0:T(8,128)} fusion(f32[8,128,1024]{2,1,0:T(8,128)} %param.7, f32[8,128,512]{2,1,0:T(8,128)S(1)} %slice.8, s32[]{:T(128)S(6)} %select_n.4), kind=kOutput, calls=%fused_computation.5 | convolution fusion | flops 402653184 | bytes 5767172 | tf_op jit(solution)/shard_map/dri,drs->dis/dot_general | solution.py:39
  336.4 0.0 all-reduce.2.cloned.1.call-update
  336.4 1.3 slice.9
  337.7 0.1 constant_dynamic-slice_fusion
  337.9 0.1 copy.24
  338.0 27.6 %all-to-all-done = f32[8,128,512]{1,0,2:T(8,128)} async-done(((f32[8,128,512]{1,0,2:T(8,128)}), f32[8,128,512]{1,0,2:T(8,128)}, u32[]{:S(2)}, u32[]{:S(2)}) %all-to-all-start) | async-done | bytes 2097184 | tf_op jit(solution)/shard_map/all_to_all | solution.py:43
  365.6 4.2 copy.18
  369.8 1.7 all_to_all.16
  371.5 55.3 %all-reduce.2.cloned.1.call-done = f32[8,32,1024]{2,1,0:T(8,128)} async-done(((f32[8,32,1024]{2,1,0:T(8,128)}), f32[8,32,1024]{2,1,0:T(8,128)}) %all-reduce.2.cloned.1.call-update) | async-done | bytes 1048592 | tf_op jit(solution)/shard_map/psum | solution.py:42
  426.8 3.7 convolution_add_fusion
Async XLA Ops:
  6.5 187.7 %copy-start = (bf16[8,2048,64]{1,2,0:T(8,128)(2,1)S(1)}, bf16[8,2048,64]{1,2,0:T(8,128)(2,1)}, u32[]{:S(2)}) copy-start(bf16[8,2048,64]{1,2,0:T(8,128)(2,1)} %param.5) | copy-start | bytes 6291460
  6.5 187.7 %all-gather.3.cloned.1.call-start = ((), (), s32[]{:S(2)}) async-start(), calls=%async_computation.2 | async-start | bytes 18874368 | tf_op jit(solution)/shard_map/all_gather | solution.py:27
  7.3 274.3 %reduce-scatter.2.cloned.1.call-start = ((), (), s32[]{:S(2)}) async-start(), calls=%async_computation.3 | async-start | bytes 3342336 | tf_op jit(solution)/shard_map/reduce_scatter | solution.py:15
  217.9 102.7 %all-gather.5.cloned.1.call-start = ((), (), s32[]{:S(2)}) async-start(), calls=%async_computation.4 | async-start | bytes 3342336 | tf_op jit(solution)/shard_map/all_gather | solution.py:16
  324.3 41.3 %all-to-all-start = ((f32[8,128,512]{1,0,2:T(8,128)}), f32[8,128,512]{1,0,2:T(8,128)}, u32[]{:S(2)}, u32[]{:S(2)}) async-start(f32[8,128,512]{1,0,2:T(8,128)} %copy.16), calls=%async_computation.1 | async-start | bytes 4194304 | tf_op jit(solution)/shard_map/all_to_all | solution.py:43
  330.5 96.3 %all-reduce.2.cloned.1.call-start = ((), (), s32[]{:S(2)}) async-start(), calls=%async_computation.5 | async-start | bytes 2097152 | tf_op jit(solution)/shard_map/psum | solution.py:42
Sparse Core Ops, SparseCore 0:
  9.6 184.5 all-gather.2
  218.0 63.5 reduce-scatter.1
  283.3 37.2 all-gather.4
  336.5 90.1 all-reduce.1
where the time goes:
time: 442 us; the launch traced here: 437 us
  waiting for transfers between devices  373 us (84%)
  matrix products  30.8 us (7%)
  between operations  13.2 us (3%)
  local copies, waits for them, and re-layouts  11.2 us (3%)
  starting transfers between devices  6.49 us (1%)
    all_gather x1, waiting for transfers between devices, shards(): fragment = lax.all_gather(weights, 'col', axis=2, tiled=True)  187 us
    reduce_scatter x1, waiting for transfers between devices, sum_by_parts(): own = lax.psum_scatter(padded, axis, scatter_dimension=0, tiled=True)  63.7 us
    psum x1, waiting for transfers between devices, shards(): left = lax.psum(left_part, 'col')  55.3 us
    all_gather x1, waiting for transfers between devices, sum_by_parts(): whole = lax.all_gather(own, axis, axis=0, tiled=True)  38.9 us
    all_to_all x1, waiting for transfers between devices, shards(): lax.all_to_all(exposure, 'col', split_axis=2, concat_axis=1, tiled=True)  27.6 us
    dot_general x1, matrix products, shards(): jnp.einsum('dak,dap->dkp', weighted, fragment, preferred_element_type=jnp...  11 us
    dot_general x1, matrix products, shards(): jnp.einsum('dar,dap->drp', loadings, fragment, preferred_element_type=jnp...  10.4 us
  transfers between devices with their start and end apart: 5, of which 5 were waited for; matrix products, arithmetic and copies ran while one was open for 3% of the time, Pallas kernels for 0%

commit v1 on v0

v1 whole, which is shorter than its diff:
```python
import jax
import jax.numpy as jnp
from jax import lax
from jax.experimental import pallas as pl
from jax.experimental.pallas import tpu as pltpu
from jax.sharding import PartitionSpec as P

MESH = pl.DeviceIdType.MESH
F32 = jnp.float32
BF16 = jnp.bfloat16
NT = (((1,), (1,)), ((), ()))
SLOT = {0: 0, 2: 1, 1: 2, 3: 3}


def kernel(load_ref, wt_ref, spec_ref, fcov_ref, out_ref,
           wt_all, l_all, wg, f_rows,
           part_s, part_o, part_n, part_f,
           send_s, send_o, send_n, send_f,
           got_s, got_o, got_n, got_f,
           rs_s, rs_o, rs_n, rs_f,
           red, s_red, s_all, e_all, left_val, left_buf, obuf, oin,
           wy_s, wy_r, ly_s, ly_r, wx_s, wx_r, loc, f_s, f_r,
           cc_s, cc_r, rss_s, rss_r, ag_s, ag_r, sx_s, sx_r, la_s, la_r, fo_s, fo_r):
    row, col = lax.axis_index("row"), lax.axis_index("col")
    z, xl, core = row // 4, (row // 2) % 2, row % 2
    y, xh = col // 2, col % 2
    ports = 2 * z + xl

    def dev(z_, xl_, core_, y_, xh_):
        return (z_ * 4 + xl_ * 2 + core_, y_ * 2 + xh_)

    def remote(src, dst, ssem, rsem, to):
        return pltpu.make_async_remote_copy(
            src_ref=src, dst_ref=dst, send_sem=ssem, recv_sem=rsem,
            device_id=to, device_id_type=MESH)

    bar = pltpu.get_barrier_semaphore()

    def greet(k, _):
        a = (core * 8 + y * 2 + xh + k) % 16
        pl.semaphore_signal(bar, inc=1, device_id=dev(z, xl, a // 8, (a // 2) % 4, a % 2), device_id_type=MESH)
        b = (z * 4 + xl * 2 + xh + k) % 16
        pl.semaphore_signal(bar, inc=1, device_id=dev(b // 4, (b // 2) % 2, core, y, b % 2), device_id_type=MESH)
        return 0

    lax.fori_loop(1, 16, greet, 0)
    pl.semaphore_wait(bar, 30)

    def at64(i):
        return pl.ds(pl.multiple_of(i * 64, 64), 64)

    def at128(i):
        return pl.ds(pl.multiple_of(i * 128, 128), 128)

    own_w = []
    for dl in range(2):
        c = pltpu.make_async_copy(wt_ref.at[2 * y + dl], wt_all.at[dl, at64(col), :], loc.at[dl])
        c.start()
        own_w.append(c)
    wy = {}
    for dl in range(2):
        for dy in (1, 3, 2):
            ty = (y + dy) % 4
            c = remote(wt_ref.at[2 * ty + dl], wt_all.at[dl, at64(col), :],
                       wy_s.at[dy - 1, dl], wy_r.at[dy - 1, dl], dev(z, xl, core, ty, xh))
            c.start()
            wy[dy, dl] = c
    wx = {}
    for dl in range(2):
        c = remote(wt_ref.at[2 * y + dl], wt_all.at[dl, at64(col), :],
                   wx_s.at[0, dl], wx_r.at[0, dl], dev(z, xl, core, y, 1 - xh))
        c.start()
        wx[0, dl] = c
    own_l = []
    for dl in range(2):
        c = pltpu.make_async_copy(load_ref.at[2 * y + dl], l_all.at[dl, :, pl.ds(0, 128)], loc.at[2 + dl])
        c.start()
        own_l.append(c)
    ly = {}
    for dy in (1, 3, 2):
        for dl in range(2):
            ty = (y + dy) % 4
            rel = 4 - dy
            c = remote(load_ref.at[2 * ty + dl], l_all.at[dl, :, pl.ds(128 * SLOT[rel], 128)],
                       ly_s.at[dy - 1, dl], ly_r.at[dy - 1, dl], dev(z, xl, core, ty, xh))
            c.start()
            ly[dy, dl] = c
    turn = jnp.where(core == 0, z, 4 - z)
    yq = (y + turn) % 4
    yd = (y + 4 - turn) % 4
    f_copy = remote(fcov_ref.at[2 * yd + core], f_rows, f_s, f_r, dev(z, xl, core, yd, xh))
    f_own = pltpu.make_async_copy(fcov_ref.at[2 * y + core], f_rows, loc.at[4])

    @pl.when(z == 0)
    def _():
        f_own.start()

    @pl.when(z != 0)
    def _():
        f_copy.start()

    for dl in range(2):
        for rel in (1, 3, 2):
            sy = (y + rel) % 4
            wy[4 - rel, dl].wait_recv()
            rows = at64(2 * sy + xh)
            c = remote(wt_all.at[dl, rows, :], wt_all.at[dl, rows, :],
                       wx_s.at[rel, dl], wx_r.at[rel, dl], dev(z, xl, core, y, 1 - xh))
            c.start()
            wx[rel, dl] = c
    for c in own_w + own_l:
        c.wait()
    for dl in range(2):
        scale = spec_ref[pl.ds(2 * y + dl, 1), :]
        for b in range(4):
            w = wt_all[dl, at64(2 * b + xh), :]
            wg[dl, pl.ds(64 * b, 64), :] = (scale * w.astype(F32)).astype(BF16)
    for dl in range(2):
        for rel in (0, 1, 3, 2):
            wx[rel, dl].wait_recv()

    mate = dev(z, xl, 1 - core, y, xh)

    def both(part, send, got, i, product):
        send[...] = product(1 - core)
        c = remote(send, got, cc_s.at[i], cc_r.at[i], mate)
        c.start()
        part[...] = product(core)
        return c

    def spread(part, got, rs, i, pair):
        pair.wait_recv()
        part[...] = part[...] + got[...]

        def go(k, _):
            to = (ports + k) % 8
            remote(part.at[at64(to), :], rs.at[k - 1], rss_s.at[i, k - 1], rss_r.at[i, k - 1],
                   dev(to // 2, to % 2, core, y, xh)).start()
            return 0

        lax.fori_loop(1, 8, go, 0)

    def rs_wait(part, rs, i):
        def one(k, _):
            remote(part.at[at64(0), :], rs.at[k], rss_s.at[i, k], rss_r.at[i, k], mate).wait_recv()
            return 0

        lax.fori_loop(0, 7, one, 0)
        total = part[at64(ports), :]
        for k in range(7):
            total = total + rs[k]
        return total

    def gather(value, u, rel):
        block = 2 * ((y + rel) % 4) + xh
        red[u] = value
        e_all[at64(ports), at128(block)] = value

        def go(k, _):
            b = (z * 4 + xl * 2 + xh + k) % 16
            remote(red.at[u], e_all.at[at64(ports), at128(block)], ag_s.at[u, k - 1], ag_r.at[u, k - 1],
                   dev(b // 4, (b // 2) % 2, core, y, b % 2)).start()
            return 0

        lax.fori_loop(1, 16, go, 0)

    def l_dot(lo, n):
        def product(d):
            return jnp.dot(wt_all[d], l_all[d, :, pl.ds(lo, n)], preferred_element_type=F32)

        return product

    def s_dot(d):
        return lax.dot_general(wt_all[d], wg[d], NT, preferred_element_type=F32)

    pair_s = both(part_s, send_s, got_s, 0, s_dot)
    pair_o = both(part_o, send_o, got_o, 1, l_dot(0, 128))
    spread(part_s, got_s, rs_s, 0, pair_s)
    spread(part_o, got_o, rs_o, 1, pair_o)
    for dy in (1, 3):
        for dl in range(2):
            ly[dy, dl].wait_recv()
    pair_n = both(part_n, send_n, got_n, 2, l_dot(256, 256))
    spread(part_n, got_n, rs_n, 2, pair_n)
    s_red[...] = rs_wait(part_s, rs_s, 0)
    mine = pl.ds(pl.multiple_of(xh * 32, 32), 32)
    theirs = pl.ds(pl.multiple_of((1 - xh) * 32, 32), 32)
    s_copy = remote(s_red.at[theirs, :], s_all.at[xh], sx_s, sx_r, dev(z, xl, core, y, 1 - xh))
    s_copy.start()
    s_all[xh] = s_red[mine, :]
    gather(rs_wait(part_o, rs_o, 1), 0, 0)
    both_n = rs_wait(part_n, rs_n, 2)
    gather(both_n[:, :128], 1, 1)
    gather(both_n[:, 128:], 2, 3)
    for dl in range(2):
        ly[2, dl].wait_recv()
    pair_f = both(part_f, send_f, got_f, 3, l_dot(128, 128))
    spread(part_f, got_f, rs_f, 3, pair_f)
    gather(rs_wait(part_f, rs_f, 3), 3, 2)

    def ag_wait(i, _):
        u, k = i // 15, i % 15
        remote(red.at[u], e_all.at[at64(0), at128(0)], ag_s.at[u, k], ag_r.at[u, k], mate).wait_recv()
        return 0

    lax.fori_loop(0, 60, ag_wait, 0)

    @pl.when(z == 0)
    def _():
        f_own.wait()

    @pl.when(z != 0)
    def _():
        f_copy.wait_recv()

    e_rows = jnp.concatenate([e_all[at64(2 * b + xl), :] for b in range(4)], axis=0)
    left_val[...] = lax.dot_general(e_rows, f_rows[...], NT, precision=lax.Precision.HIGHEST,
                                    preferred_element_type=F32)
    block = 2 * yq + xh
    me8 = 2 * z + xh

    def rows32(i):
        return pl.ds(pl.multiple_of(i * 32, 32), 32)

    def la(k):
        to = (me8 + k) % 8
        return remote(left_val.at[rows32(to), :], left_buf.at[:, at128(block)], la_s.at[k - 1], la_r.at[k - 1],
                      dev(to // 2, xl, core, y, to % 2))

    def la_go(k, _):
        la(k).start()
        return 0

    lax.fori_loop(1, 8, la_go, 0)
    left_buf[:, at128(block)] = left_val[rows32(me8), :]

    def la_wait(k, _):
        la(k).wait_recv()
        return 0

    lax.fori_loop(1, 8, la_wait, 0)
    factor = lax.dot_general(left_buf[...], e_all[...], NT, precision=lax.Precision.HIGHEST,
                             preferred_element_type=F32)
    s_copy.wait_recv()
    for c in range(8):
        obuf[c] = factor[:, 64 * c:64 * c + 64] + s_all[c % 2, :, 64 * (c // 2):64 * (c // 2) + 64]
    day = 2 * y + core
    base = core * 8 + y * 2 + xh
    goal = xh * 8

    def fo(c):
        return remote(obuf.at[c], oin.at[day], fo_s.at[c], fo_r.at[day], dev(z, xl, xh, c // 2, c % 2))

    def fo_go(c, _):
        @pl.when(goal + c != base)
        def _():
            fo(c).start()

        return 0

    lax.fori_loop(0, 8, fo_go, 0)

    @pl.when(xh == core)
    def _():
        oin[day] = obuf[col]

    def fo_wait(d, _):
        @pl.when((d % 2) * 8 + (d // 2) * 2 + core != base)
        def _():
            remote(obuf.at[0], oin.at[d], fo_s.at[0], fo_r.at[d], mate).wait_recv()

        return 0

    lax.fori_loop(0, 8, fo_wait, 0)
    out_ref[...] = oin[...]

    for c in [*wy.values(), *wx.values(), *ly.values(), pair_s, pair_o, pair_n, pair_f, s_copy]:
        c.wait_send()

    @pl.when(z != 0)
    def _():
        f_copy.wait_send()

    for i, (part, rs) in enumerate(((part_s, rs_s), (part_o, rs_o), (part_n, rs_n), (part_f, rs_f))):
        def rs_sent(k, _, part=part, rs=rs, i=i):
            remote(part.at[at64(0), :], rs.at[k], rss_s.at[i, k], rss_r.at[i, k], mate).wait_send()
            return 0

        lax.fori_loop(0, 7, rs_sent, 0)

    def ag_sent(i, _):
        u, k = i // 15, i % 15
        remote(red.at[u], e_all.at[at64(0), at128(0)], ag_s.at[u, k], ag_r.at[u, k], mate).wait_send()
        return 0

    lax.fori_loop(0, 60, ag_sent, 0)

    def la_sent(k, _):
        la(k).wait_send()
        return 0

    lax.fori_loop(1, 8, la_sent, 0)

    def fo_sent(c, _):
        @pl.when(goal + c != base)
        def _():
            fo(c).wait_send()

        return 0

    lax.fori_loop(0, 8, fo_sent, 0)


def shards(loadings, weights, specific, factor_cov):
    assets = loadings.shape[1]
    wt = jnp.swapaxes(weights, 1, 2)
    any_ = pl.BlockSpec(memory_space=pl.ANY)
    vmem = pl.BlockSpec(memory_space=pltpu.VMEM)
    dma = pltpu.SemaphoreType.DMA
    widths = (256, 128, 256, 128)
    return pl.pallas_call(
        kernel,
        out_shape=jax.ShapeDtypeStruct((8, 32, 64), F32),
        in_specs=[any_, any_, vmem, any_],
        out_specs=vmem,
        scratch_shapes=[
            pltpu.VMEM((2, 512, assets), BF16),
            pltpu.VMEM((2, assets, 512), BF16),
            pltpu.VMEM((2, 256, assets), BF16),
            pltpu.VMEM((128, 1024), F32),
            *[pltpu.VMEM((512, w), F32) for w in widths],
            *[pltpu.VMEM((512, w), F32) for w in widths],
            *[pltpu.VMEM((512, w), F32) for w in widths],
            *[pltpu.VMEM((7, 64, w), F32) for w in widths],
            pltpu.VMEM((4, 64, 128), F32),
            pltpu.VMEM((64, 256), F32),
            pltpu.VMEM((2, 32, 256), F32),
            pltpu.VMEM((512, 1024), F32),
            pltpu.VMEM((256, 128), F32),
            pltpu.VMEM((32, 1024), F32),
            pltpu.VMEM((8, 32, 64), F32),
            pltpu.VMEM((8, 32, 64), F32),
            dma((3, 2)), dma((3, 2)), dma((3, 2)), dma((3, 2)), dma((4, 2)), dma((4, 2)), dma((5,)), dma, dma,
            dma((4,)), dma((4,)), dma((4, 7)), dma((4, 7)), dma((4, 15)), dma((4, 15)), dma, dma,
            dma((7,)), dma((7,)), dma((8,)), dma((8,)),
        ],
        compiler_params=pltpu.CompilerParams(collective_id=0, has_side_effects=True),
    )(loadings, wt, specific, factor_cov)


def solution(mesh):
    in_specs = (P(None, "row", "col"), P(None, "row", "col"), P(None, "row"), P(None, "col", None))
    out_specs = P(None, "row", "col")
    return jax.shard_map(shards, mesh=mesh, in_specs=in_specs, out_specs=out_specs, check_vma=False)
```

time: 442 us -> 141 us (0.32)
  waiting for transfers between devices: 373 us -> 0 us
  Pallas kernels: 0 us -> 139 us
  matrix products: 30.8 us -> 0 us
  between operations: 13.2 us -> 0.01 us
  local copies, waits for them, and re-layouts: 11.2 us -> 1.57 us
  starting transfers between devices: 6.49 us -> 0 us
    all_gather x2 -> x0, waiting for transfers between devices: 226 us -> none  [the longest x1 187 us: shards(): fragment = lax.all_gather(weights, 'col', axis=2, tiled=True)]
    pallas_call x0 -> x1, Pallas kernels: none -> 139 us  [shards(): pl.pallas_call(kernel, out_shape=jax.ShapeDtypeStruct((8, 32, 64), F32),...]
    reduce_scatter x1 -> x0, waiting for transfers between devices: 63.7 us -> none  [sum_by_parts(): own = lax.psum_scatter(padded, axis, scatter_dimension=0, tiled=True)]
    psum x1 -> x0, waiting for transfers between devices: 55.3 us -> none  [shards(): left = lax.psum(left_part, 'col')]
    dot_general x4 -> x0, matrix products: 30.8 us -> none  [the longest x1 11 us: shards(): jnp.einsum('dak,dap->dkp', weighted, fragment, preferred_element_type=jnp...]
    all_to_all x1 -> x0, waiting for transfers between devices: 27.6 us -> none  [shards(): lax.all_to_all(exposure, 'col', split_axis=2, concat_axis=1, tiled=True)]
    all_to_all x1 -> x0, starting transfers between devices: 6.19 us -> none  [shards(): lax.all_to_all(exposure, 'col', split_axis=2, concat_axis=1, tiled=True)]
    all_to_all x2 -> x0, local copies, waits for them, and re-layouts: 5.88 us -> none  [shards(): lax.all_to_all(exposure, 'col', split_axis=2, concat_axis=1, tiled=True)]
  transfers between devices with their start and end apart: 5 -> 0, of which waited for: 5 -> 0; matrix products, arithmetic and copies ran while one was open for 3% -> 0% of each run, Pallas kernels for 0% -> 0%
where the time goes in v1:
time: 141 us; the launch traced here: 140 us
  Pallas kernels  139 us (99%)
  local copies, waits for them, and re-layouts  1.57 us (1%)
    pallas_call x1, Pallas kernels, shards(): pl.pallas_call(kernel, out_shape=jax.ShapeDtypeStruct((8, 32, 64), F32),...  139 us

profile of v1, /device:TPU:1, one launch (start us, length us, event | category | flops | bytes accessed | tf_op | source)
XLA Modules:
  0.0 140.4 jit_solution(9126720502703417905)
XLA Ops:
  0.0 138.9 %shard_map.46 = f32[8,32,64]{2,1,0:T(8,128)} custom-call(bf16[8,2048,128]{2,1,0:T(8,128)(2,1)} %load_ref.1, bf16[8,64,2048]{2,1,0:T(8,128)(2,1)} %bitcast.1, f32[8,2048]{1,0:T(8,128)} %spec_ref.1, f32[8,128,1024]{2,1,0:T(8,128)} %fcov_ref.1), custom_call_target="tpu_custom_call" | custom-call | tf_op jit(solution)/shard_map/pallas_call | solution.py:321
  138.9 1.6 %copy.6 = f32[8,32,64]{2,1,0:T(8,128)} copy(f32[8,32,64]{2,1,0:T(8,128)} %shard_map.46) | data formatting | bytes 131072

commit v2 on v0

v2 whole, which is shorter than its diff:
```python
import jax
import jax.numpy as jnp
from jax import lax
from jax.experimental import pallas as pl
from jax.experimental.pallas import tpu as pltpu
from jax.sharding import PartitionSpec as P

MESH = pl.DeviceIdType.MESH
F32 = jnp.float32
BF16 = jnp.bfloat16
HIGH = lax.Precision.HIGHEST
NT = (((1,), (1,)), ((), ()))
SLOT = {0: 0, 2: 1, 1: 2, 3: 3}


def kernel(load_ref, wt_ref, spec_ref, fcov_ref, out_ref,
           wt_all, l_all, w_pass, l_pass, wg, f_rows,
           part_o, part_f, part_s, send_o, send_f, send_s, got_o, got_f, got_s,
           xg_o, xg_f, xg_s, zg_o, zg_f, zg_s,
           two, got_n, rs_n, red, s_red, s_tile, e_all, left_val, left_buf, obuf, oin,
           wy_s, wy_r, ly_s, ly_r, wx_s, wx_r, wf_s, wf_r, lf_s, lf_r, loc, f_s, f_r,
           cc_s, cc_r, xl_s, xl_r, zz_s, zz_r, rn_s, rn_r, ag_s, ag_r, sx_s, sx_r,
           la_s, la_r, fo_s, fo_r):
    row, col = lax.axis_index("row"), lax.axis_index("col")
    z, xl, core = row // 4, (row // 2) % 2, row % 2
    y, xh = col // 2, col % 2
    day = 2 * y + core

    def dev(z_, xl_, core_, y_, xh_):
        return (z_ * 4 + xl_ * 2 + core_, y_ * 2 + xh_)

    def remote(src, dst, ssem, rsem, to):
        return pltpu.make_async_remote_copy(
            src_ref=src, dst_ref=dst, send_sem=ssem, recv_sem=rsem,
            device_id=to, device_id_type=MESH)

    def loop(lo, hi, body):
        def step(k, _):
            body(k)
            return 0

        lax.fori_loop(lo, hi, step, 0)

    def part64(i):
        return pl.ds(pl.multiple_of(i * 64, 64), 64)

    def lanes128(i):
        return pl.ds(pl.multiple_of(i * 128, 128), 128)

    def lanes256(i):
        return pl.ds(pl.multiple_of(i * 256, 256), 256)

    bar = pltpu.get_barrier_semaphore()

    def greet(to):
        pl.semaphore_signal(bar, inc=1, device_id=to, device_id_type=MESH)

    def greet_line(k):
        a = (core * 4 + y + k) % 8
        greet(dev(z, xl, a // 4, a % 4, xh))

    def greet_plane(k):
        b = (z * 4 + xl * 2 + xh + k) % 16
        greet(dev(b // 4, (b // 2) % 2, core, y, b % 2))

    def greet_swap(k):
        greet(dev(z, xh, k // 4, k % 4, xl))

    loop(1, 8, greet_line)
    loop(1, 16, greet_plane)

    @pl.when(xl != xh)
    def _():
        loop(0, 8, greet_swap)
        pl.semaphore_wait(bar, 30)

    @pl.when(xl == xh)
    def _():
        pl.semaphore_wait(bar, 22)

    def block_of(b):
        return part64(4 * xh + b)

    here = block_of(y)
    across = dev(z, xl, core, y, 1 - xh)
    near = (1, 3)
    own = []
    wy, wx, ly, wf, lf = {}, {}, {}, {}, {}

    def w_near(dy, dl):
        ty = (y + dy) % 4
        wy[dy, dl] = remote(wt_ref.at[2 * ty + dl], wt_all.at[dl, here, :],
                            wy_s.at[dy - 1, dl], wy_r.at[dy - 1, dl], dev(z, xl, core, ty, xh))
        wy[dy, dl].start()

    def w_across(rel, dl):
        rows = block_of((y + rel) % 4)
        src = wt_ref.at[2 * y + dl] if rel == 0 else wt_all.at[dl, rows, :]
        wx[rel, dl] = remote(src, wt_all.at[dl, rows, :], wx_s.at[rel, dl], wx_r.at[rel, dl], across)
        wx[rel, dl].start()

    def w_arrived(rel, dl):
        wy[4 - rel, dl].wait_recv()
        w_across(rel, dl)

    def l_near(dy, dl):
        ty = (y + dy) % 4
        ly[dy, dl] = remote(load_ref.at[2 * ty + dl], l_all.at[dl, :, pl.ds(128 * SLOT[4 - dy], 128)],
                            ly_s.at[dy - 1, dl], ly_r.at[dy - 1, dl], dev(z, xl, core, ty, xh))
        ly[dy, dl].start()

    for dy in near:
        w_near(dy, 0)
    for dl in range(2):
        w_across(0, dl)
        own.append(pltpu.make_async_copy(wt_ref.at[2 * y + dl], wt_all.at[dl, here, :], loc.at[dl]))
        own[-1].start()
    for dl in range(2):
        wf[dl] = remote(wt_ref.at[2 * ((y + 2) % 4) + dl], w_pass.at[dl], wf_s.at[dl], wf_r.at[dl],
                        dev(z, xl, core, (y + near[dl]) % 4, xh))
        wf[dl].start()
    for dy in near:
        w_near(dy, 1)
    for dl in range(2):
        own.append(pltpu.make_async_copy(load_ref.at[2 * y + dl], l_all.at[dl, :, pl.ds(0, 128)], loc.at[2 + dl]))
        own[-1].start()
    w_arrived(1, 0)
    w_arrived(3, 0)
    for dl in range(2):
        wf[dl].wait_recv()
        wy[2, dl] = remote(w_pass.at[dl], wt_all.at[dl, block_of((y + near[1 - dl]) % 4), :],
                           wy_s.at[1, dl], wy_r.at[1, dl], dev(z, xl, core, (y + near[dl]) % 4, xh))
        wy[2, dl].start()
    for dl in range(2):
        lf[dl] = remote(load_ref.at[2 * ((y + 2) % 4) + dl], l_pass.at[dl], lf_s.at[dl], lf_r.at[dl],
                        dev(z, xl, core, (y + near[dl]) % 4, xh))
        lf[dl].start()
    for dy in near:
        l_near(dy, 0)
    w_arrived(1, 1)
    w_arrived(3, 1)
    w_arrived(2, 0)
    w_arrived(2, 1)
    for c in own:
        c.wait()
    for dl in range(2):
        scale = spec_ref[pl.ds(2 * y + dl, 1), :]
        w = wt_all[dl, lanes256(xh), :]
        wg[dl] = (scale * w.astype(F32)).astype(BF16)
    for dl in range(2):
        lf[dl].wait_recv()
        ly[2, dl] = remote(l_pass.at[dl], l_all.at[dl, :, pl.ds(128 * SLOT[2], 128)],
                           ly_s.at[1, dl], ly_r.at[1, dl], dev(z, xl, core, (y + near[dl]) % 4, xh))
        ly[2, dl].start()
    for dy in near:
        l_near(dy, 1)
    turn = (z + 2 * core) % 4
    yq = (y + turn) % 4
    yd = (y + 4 - turn) % 4
    f_copy = remote(fcov_ref.at[2 * yd + core], f_rows, f_s, f_r, dev(z, xl, core, yd, xh))
    f_own = pltpu.make_async_copy(fcov_ref.at[day], f_rows, loc.at[4])

    @pl.when(turn == 0)
    def _():
        f_own.start()

    @pl.when(turn != 0)
    def _():
        f_copy.start()

    for dl in range(2):
        for rel in (0, 1, 3, 2):
            wx[rel, dl].wait_recv()
    mate = dev(z, xl, 1 - core, y, xh)
    beside = dev(z, 1 - xl, core, y, xh)
    kept, given = lanes256(xl), lanes256(1 - xl)

    def l_dot(lo, n):
        def product(d):
            return jnp.dot(wt_all[d], l_all[d, :, pl.ds(lo, n)], preferred_element_type=F32)

        return product

    def s_dot(d):
        return lax.dot_general(wt_all[d], wg[d], NT, preferred_element_type=F32)

    class Group:
        def __init__(self, i, part, send, got, xg, zg, product):
            self.i, self.part, self.send, self.got, self.xg, self.zg = i, part, send, got, xg, zg
            self.product = product
            self.pair = remote(send, got, cc_s.at[i], cc_r.at[i], mate)
            self.side = remote(part.at[given, :], xg, xl_s.at[i], xl_r.at[i], beside)

        def dots(self):
            self.send[...] = self.product(1 - core)
            self.pair.start()
            self.part[...] = self.product(core)

        def over_x(self):
            self.pair.wait_recv()
            self.part[given, :] = self.part[given, :] + self.got[given, :]
            self.side.start()
            self.part[kept, :] = self.part[kept, :] + self.got[kept, :]

        def line(self, k):
            to = (z + k) % 4
            return remote(self.xg.at[part64(to), :], self.zg.at[k - 1],
                          zz_s.at[self.i, k - 1], zz_r.at[self.i, k - 1], dev(to, xl, core, y, xh))

        def over_z(self):
            self.side.wait_recv()
            self.xg[...] = self.xg[...] + self.part[kept, :]
            for k in (1, 3, 2):
                self.line(k).start()

        def total(self):
            for k in (1, 3, 2):
                self.line(k).wait_recv()
            return (self.xg[part64(z), :] + self.zg[0]) + (self.zg[1] + self.zg[2])

        def sent(self):
            self.pair.wait_send()
            self.side.wait_send()
            for k in (1, 3, 2):
                self.line(k).wait_send()

    me8 = 2 * z + xh

    def spread(u, k, block):
        b = (me8 + k) % 8
        return remote(red.at[u], e_all.at[part64(z), lanes128(block)], ag_s.at[u, k - 1], ag_r.at[u, k - 1],
                      dev(b // 2, xl, core, y, b % 2))

    def gather(value, u, rel):
        block = 2 * ((y + rel) % 4) + xh
        red[u] = value
        loop(1, 8, lambda k: spread(u, k, block).start())
        e_all[part64(z), lanes128(block)] = value

    g_o = Group(0, part_o, send_o, got_o, xg_o, zg_o, l_dot(0, 128))
    g_f = Group(1, part_f, send_f, got_f, xg_f, zg_f, l_dot(128, 128))
    g_s = Group(2, part_s, send_s, got_s, xg_s, zg_s, s_dot)

    me_p = 4 * xl + z

    def pair_n(dl):
        return remote(two.at[dl], got_n, cc_s.at[3], cc_r.at[3], mate)

    def rn(k):
        p = (me_p + k) % 8
        return remote(two.at[core, part64(p), :], rs_n.at[k - 1], rn_s.at[k - 1], rn_r.at[k - 1],
                      dev(p % 4, p // 4, core, y, xh))

    def near_dot(dl):
        for dy in near:
            ly[dy, dl].wait_recv()
        two[dl] = jnp.dot(wt_all[dl], l_all[dl, :, pl.ds(256, 256)], preferred_element_type=F32)

        @pl.when(core != dl)
        def _():
            pair_n(dl).start()

    def near_add(dl):
        @pl.when(core == dl)
        def _():
            pair_n(dl).wait_recv()
            two[dl] = two[dl] + got_n[...]
            loop(1, 8, lambda k: rn(k).start())

    def near_gather(dl):
        @pl.when(core == dl)
        def _():
            loop(1, 8, lambda k: rn(k).wait_recv())
            total = two[dl, part64(me_p), :]
            for k in range(7):
                total = total + rs_n[k]
            gather(total[:, :128], 2, 1)
            gather(total[:, 128:], 3, 3)

    g_o.dots()
    g_o.over_x()
    near_dot(0)
    g_s.dots()
    g_o.over_z()
    near_add(0)
    g_s.over_x()
    gather(g_o.total(), 0, 0)
    for dl in range(2):
        ly[2, dl].wait_recv()
    g_f.dots()
    g_f.over_x()
    g_s.over_z()
    near_gather(0)
    g_f.over_z()
    swap = remote(s_red, s_tile, sx_s, sx_r, dev(z, xh, core, y, xl))
    s_red[...] = g_s.total()

    @pl.when(xl != xh)
    def _():
        swap.start()

    @pl.when(xl == xh)
    def _():
        s_tile[...] = s_red[...]

    for c in [*wy.values(), *wx.values(), *wf.values()]:
        c.wait_send()
    gather(g_f.total(), 1, 2)
    near_dot(1)
    near_add(1)

    @pl.when(turn == 0)
    def _():
        f_own.wait()

    @pl.when(turn != 0)
    def _():
        f_copy.wait_recv()

    def left_part(u, rel):
        loop(1, 8, lambda k: spread(u, k, 0).wait_recv())
        at = lanes256((y + rel) % 4)
        return lax.dot_general(e_all[:, at], f_rows[:, at], NT, precision=HIGH, preferred_element_type=F32)

    left_val[...] = left_part(0, 0) + left_part(1, 2)
    for g in (g_o, g_f, g_s):
        g.sent()
    near_gather(1)
    left_val[...] += left_part(2, 1) + left_part(3, 3)

    def la(j):
        return remote(left_val.at[part64(j // 2), :], left_buf.at[:, lanes128(2 * yq + xh)],
                      la_s.at[j], la_r.at[me8], dev(j // 2, j % 2, core, y, xl))

    alike = xl == xh
    me_t = 2 * z + xl

    def unless(skip, body):
        @pl.when(jnp.logical_not(skip))
        def _():
            body()

    loop(0, 8, lambda j: unless(jnp.logical_and(alike, j == me_t), lambda: la(j).start()))

    @pl.when(alike)
    def _():
        left_buf[:, lanes128(2 * yq + xh)] = left_val[part64(z), :]

    for u in range(4):
        loop(1, 8, lambda k, u=u: spread(u, k, 0).wait_send())
    loop(1, 8, lambda k: rn(k).wait_send())

    def la_in(j):
        return remote(left_val.at[part64(0), :], left_buf.at[:, lanes128(0)], la_s.at[0], la_r.at[j], mate)

    loop(0, 8, lambda j: unless(jnp.logical_and(alike, j == me8), lambda: la_in(j).wait_recv()))
    tile = lax.dot_general(left_buf[...], e_all[...], NT, precision=HIGH, preferred_element_type=F32)

    @pl.when(xl != xh)
    def _():
        swap.wait_recv()

    tile = tile + s_tile[...]
    for h in range(2):
        for b in range(4):
            obuf[4 * h + b] = tile[32 * h:32 * h + 32, 64 * b:64 * b + 64]

    def fo(i):
        return remote(obuf.at[i], oin.at[day], fo_s.at[i], fo_r.at[day], dev(z, xh, i // 4, i % 4, xl))

    me_o = 4 * core + y
    loop(0, 8, lambda i: unless(jnp.logical_and(alike, i == me_o), lambda: fo(i).start()))

    @pl.when(alike)
    def _():
        oin[day] = obuf[me_o]

    for c in [*ly.values(), *lf.values()]:
        c.wait_send()
    pair_n(1 - core).wait_send()

    @pl.when(xl != xh)
    def _():
        swap.wait_send()

    @pl.when(turn != 0)
    def _():
        f_copy.wait_send()

    loop(0, 8, lambda j: unless(jnp.logical_and(alike, j == me_t), lambda: la(j).wait_send()))

    def fo_in(d):
        return remote(obuf.at[0], oin.at[d], fo_s.at[0], fo_r.at[d], mate)

    loop(0, 8, lambda d: unless(jnp.logical_and(alike, d == day), lambda: fo_in(d).wait_recv()))
    out_ref[...] = oin[...]
    loop(0, 8, lambda i: unless(jnp.logical_and(alike, i == me_o), lambda: fo(i).wait_send()))


def shards(loadings, weights, specific, factor_cov):
    assets = loadings.shape[1]
    wt = jnp.swapaxes(weights, 1, 2)
    any_ = pl.BlockSpec(memory_space=pl.ANY)
    vmem = pl.BlockSpec(memory_space=pltpu.VMEM)
    dma = pltpu.SemaphoreType.DMA
    widths = (128, 128, 256)
    return pl.pallas_call(
        kernel,
        out_shape=jax.ShapeDtypeStruct((8, 32, 64), F32),
        in_specs=[any_, any_, vmem, any_],
        out_specs=vmem,
        scratch_shapes=[
            pltpu.VMEM((2, 512, assets), BF16),
            pltpu.VMEM((2, assets, 512), BF16),
            pltpu.VMEM((2, 64, assets), BF16),
            pltpu.VMEM((2, assets, 128), BF16),
            pltpu.VMEM((2, 256, assets), BF16),
            pltpu.VMEM((128, 1024), F32),
            *[pltpu.VMEM((512, w), F32) for w in widths],
            *[pltpu.VMEM((512, w), F32) for w in widths],
            *[pltpu.VMEM((512, w), F32) for w in widths],
            *[pltpu.VMEM((256, w), F32) for w in widths],
            *[pltpu.VMEM((3, 64, w), F32) for w in widths],
            pltpu.VMEM((2, 512, 256), F32),
            pltpu.VMEM((512, 256), F32),
            pltpu.VMEM((7, 64, 256), F32),
            pltpu.VMEM((4, 64, 128), F32),
            pltpu.VMEM((64, 256), F32),
            pltpu.VMEM((64, 256), F32),
            pltpu.VMEM((256, 1024), F32),
            pltpu.VMEM((256, 128), F32),
            pltpu.VMEM((64, 1024), F32),
            pltpu.VMEM((8, 32, 64), F32),
            pltpu.VMEM((8, 32, 64), F32),
            dma((3, 2)), dma((3, 2)), dma((3, 2)), dma((3, 2)), dma((4, 2)), dma((4, 2)),
            dma((2,)), dma((2,)), dma((2,)), dma((2,)), dma((5,)), dma, dma,
            dma((4,)), dma((4,)), dma((3,)), dma((3,)), dma((3, 3)), dma((3, 3)), dma((7,)), dma((7,)),
            dma((4, 7)), dma((4, 7)), dma, dma, dma((8,)), dma((8,)), dma((8,)), dma((8,)),
        ],
        compiler_params=pltpu.CompilerParams(collective_id=0, has_side_effects=True),
    )(loadings, wt, specific, factor_cov)


def solution(mesh):
    in_specs = (P(None, "row", "col"), P(None, "row", "col"), P(None, "row"), P(None, "col", None))
    out_specs = P(None, "row", "col")
    return jax.shard_map(shards, mesh=mesh, in_specs=in_specs, out_specs=out_specs, check_vma=False)
```

time: 442 us -> 117 us (0.26); the launches traced: 437 us -> 117 us
  waiting for transfers between devices: 373 us -> 0 us
  Pallas kernels: 0 us -> 115 us
  matrix products: 30.8 us -> 0 us
  between operations: 13.2 us -> 0.01 us
  local copies, waits for them, and re-layouts: 11.2 us -> 1.57 us
  starting transfers between devices: 6.49 us -> 0 us
    all_gather x2 -> x0, waiting for transfers between devices: 226 us -> none  [the longest x1 187 us: shards(): fragment = lax.all_gather(weights, 'col', axis=2, tiled=True)]
    pallas_call x0 -> x1, Pallas kernels: none -> 115 us  [shards(): pl.pallas_call(kernel, out_shape=jax.ShapeDtypeStruct((8, 32, 64), F32),...]
    reduce_scatter x1 -> x0, waiting for transfers between devices: 63.7 us -> none  [sum_by_parts(): own = lax.psum_scatter(padded, axis, scatter_dimension=0, tiled=True)]
    psum x1 -> x0, waiting for transfers between devices: 55.3 us -> none  [shards(): left = lax.psum(left_part, 'col')]
    dot_general x4 -> x0, matrix products: 30.8 us -> none  [the longest x1 11 us: shards(): jnp.einsum('dak,dap->dkp', weighted, fragment, preferred_element_type=jnp...]
    all_to_all x1 -> x0, waiting for transfers between devices: 27.6 us -> none  [shards(): lax.all_to_all(exposure, 'col', split_axis=2, concat_axis=1, tiled=True)]
    all_to_all x1 -> x0, starting transfers between devices: 6.19 us -> none  [shards(): lax.all_to_all(exposure, 'col', split_axis=2, concat_axis=1, tiled=True)]
    all_to_all x2 -> x0, local copies, waits for them, and re-layouts: 5.88 us -> none  [shards(): lax.all_to_all(exposure, 'col', split_axis=2, concat_axis=1, tiled=True)]
  transfers between devices with their start and end apart: 5 -> 0, of which waited for: 5 -> 0; matrix products, arithmetic and copies ran while one was open for 3% -> 0% of each run, Pallas kernels for 0% -> 0%
where the time goes in v2:
time: 117 us
  Pallas kernels  115 us (98%)
  local copies, waits for them, and re-layouts  1.57 us (1%)
    pallas_call x1, Pallas kernels, shards(): pl.pallas_call(kernel, out_shape=jax.ShapeDtypeStruct((8, 32, 64), F32),...  115 us

profile of v2, /device:TPU:1, one launch (start us, length us, event | category | flops | bytes accessed | tf_op | source)
XLA Modules:
  0.0 116.7 jit_solution(8905818300019140743)
XLA Ops:
  0.0 115.1 %shard_map.46 = f32[8,32,64]{2,1,0:T(8,128)} custom-call(bf16[8,2048,128]{2,1,0:T(8,128)(2,1)} %load_ref.1, bf16[8,64,2048]{2,1,0:T(8,128)(2,1)} %bitcast.1, f32[8,2048]{1,0:T(8,128)} %spec_ref.1, f32[8,128,1024]{2,1,0:T(8,128)} %fcov_ref.1), custom_call_target="tpu_custom_call" | custom-call | tf_op jit(solution)/shard_map/pallas_call | solution.py:407
  115.1 1.6 %copy.6 = f32[8,32,64]{2,1,0:T(8,128)} copy(f32[8,32,64]{2,1,0:T(8,128)} %shard_map.46) | data formatting | bytes 131072

commit v3 on v2

--- a/solution.py
+++ b/solution.py
@@ -8,18 +8,32 @@
 MESH = pl.DeviceIdType.MESH
 F32 = jnp.float32
 BF16 = jnp.bfloat16
-HIGH = lax.Precision.HIGHEST
 NT = (((1,), (1,)), ((), ()))
 SLOT = {0: 0, 2: 1, 1: 2, 3: 3}
+OTHERS = ((2, 1), (1, 1), (3, 1), (2, 0), (1, 0), (3, 0), (0, 1))
+
+
+def halves(value):
+    top = value.astype(BF16)
+    return top, (value - top.astype(F32)).astype(BF16)
+
+
+def dot_nt(a, b):
+    (a_top, a_low), (b_top, b_low) = halves(a), halves(b)
+
+    def one(p, q):
+        return lax.dot_general(p, q, NT, preferred_element_type=F32)
+
+    return one(a_top, b_top) + (one(a_top, b_low) + one(a_low, b_top))
 
 
 def kernel(load_ref, wt_ref, spec_ref, fcov_ref, out_ref,
            wt_all, l_all, w_pass, l_pass, wg, f_rows,
-           part_o, part_f, part_s, send_o, send_f, send_s, got_o, got_f, got_s,
-           xg_o, xg_f, xg_s, zg_o, zg_f, zg_s,
+           part_o, send_o, got_o, xg_o, zg_o, part_f, send_f, got_f, rs_f,
+           part_s, send_s, got_s, zg_s, sum_s, in_s,
            two, got_n, rs_n, red, s_red, s_tile, e_all, left_val, left_buf, obuf, oin,
            wy_s, wy_r, ly_s, ly_r, wx_s, wx_r, wf_s, wf_r, lf_s, lf_r, loc, f_s, f_r,
-           cc_s, cc_r, xl_s, xl_r, zz_s, zz_r, rn_s, rn_r, ag_s, ag_r, sx_s, sx_r,
+           cc_s, cc_r, xl_s, xl_r, zz_s, zz_r, rf_s, rf_r, rn_s, rn_r, ag_s, ag_r, sx_s, sx_r, sd_s, sd_r, sl_s, sl_r, sc_s, sc_r,
            la_s, la_r, fo_s, fo_r):
     row, col = lax.axis_index("row"), lax.axis_index("col")
     z, xl, core = row // 4, (row // 2) % 2, row % 2
@@ -147,6 +161,110 @@
         scale = spec_ref[pl.ds(2 * y + dl, 1), :]
         w = wt_all[dl, lanes256(xh), :]
         wg[dl] = (scale * w.astype(F32)).astype(BF16)
+    mate = dev(z, xl, 1 - core, y, xh)
+    beside = dev(z, 1 - xl, core, y, xh)
+    kept, given = lanes256(xl), lanes256(1 - xl)
+
+    def l_dot(lo, n):
+        def product(d):
+            return jnp.dot(wt_all[d], l_all[d, :, pl.ds(lo, n)], preferred_element_type=F32)
+
+        return product
+
+    class Group:
+        def __init__(self, i, part, send, got, xg, zg, product):
+            self.i, self.part, self.send, self.got, self.xg, self.zg = i, part, send, got, xg, zg
+            self.product = product
+            self.pair = remote(send, got, cc_s.at[i], cc_r.at[i], mate)
+            self.side = remote(part.at[given, :], xg, xl_s.at[i], xl_r.at[i], beside)
+
+        def dots(self):
+            self.send[...] = self.product(1 - core)
+            self.pair.start()
+            self.part[...] = self.product(core)
+
+        def over_x(self):
+            self.pair.wait_recv()
+            self.part[given, :] = self.part[given, :] + self.got[given, :]
+            self.side.start()
+            self.part[kept, :] = self.part[kept, :] + self.got[kept, :]
+
+        def line(self, k):
+            to = (z + k) % 4
+            return remote(self.xg.at[part64(to), :], self.zg.at[k - 1],
+                          zz_s.at[self.i, k - 1], zz_r.at[self.i, k - 1], dev(to, xl, core, y, xh))
+
+        def over_z(self):
+            self.side.wait_recv()
+            self.xg[...] = self.xg[...] + self.part[kept, :]
+            for k in (1, 3, 2):
+                self.line(k).start()
+
+        def total(self):
+            for k in (1, 3, 2):
+                self.line(k).wait_recv()
+            return (self.xg[part64(z), :] + self.zg[0]) + (self.zg[1] + self.zg[2])
+
+        def sent(self):
+            self.pair.wait_send()
+            self.side.wait_send()
+            for k in (1, 3, 2):
+                self.line(k).wait_send()
+
+    alike = xl == xh
+    differ = xl != xh
+
+    class Specific:
+        def __init__(self, i, rows, keep, give):
+            self.i, self.rows, self.keep, self.give = i, rows, keep, give
+            self.pair = remote(send_s.at[i], got_s.at[i], sc_s.at[i], sc_r.at[i], mate)
+            self.side = remote(sum_s.at[i], in_s.at[i], sd_s.at[i], sd_r.at[i], beside)
+
+        def product(self, d):
+            return lax.dot_general(wt_all[d, self.rows, :], wg[d], NT, preferred_element_type=F32)
+
+        def dots(self):
+            send_s[self.i] = self.product(1 - core)
+            self.pair.start()
+            part_s[self.i] = self.product(core)
+
+        def line(self, k):
+            to = (z + k) % 4
+            return remote(part_s.at[self.i, part64(to), :], zg_s.at[self.i, k - 1],
+                          sl_s.at[self.i, k - 1], sl_r.at[self.i, k - 1], dev(to, xl, core, y, xh))
+
+        def over_z(self):
+            self.pair.wait_recv()
+            part_s[self.i] = part_s[self.i] + got_s[self.i]
+            for k in (2, 1, 3):
+                self.line(k).start()
+
+        def over_x(self):
+            for k in (1, 3, 2):
+                self.line(k).wait_recv()
+            i = self.i
+            sum_s[i] = (part_s[i, part64(z), :] + zg_s[i, 0]) + (zg_s[i, 1] + zg_s[i, 2])
+
+            @pl.when(self.give)
+            def _():
+                self.side.start()
+
+        def total(self):
+            self.side.wait_recv()
+            return sum_s[self.i] + in_s[self.i]
+
+        def sent(self):
+            self.pair.wait_send()
+            for k in (1, 3, 2):
+                self.line(k).wait_send()
+
+            @pl.when(self.give)
+            def _():
+                self.side.wait_send()
+
+    g_s = Specific(0, lanes256(xh), alike, differ)
+    g_s.dots()
+    g_s.over_z()
     for dl in range(2):
         lf[dl].wait_recv()
         ly[2, dl] = remote(l_pass.at[dl], l_all.at[dl, :, pl.ds(128 * SLOT[2], 128)],
@@ -160,154 +278,166 @@
     f_copy = remote(fcov_ref.at[2 * yd + core], f_rows, f_s, f_r, dev(z, xl, core, yd, xh))
     f_own = pltpu.make_async_copy(fcov_ref.at[day], f_rows, loc.at[4])
 
-    @pl.when(turn == 0)
-    def _():
-        f_own.start()
-
-    @pl.when(turn != 0)
-    def _():
-        f_copy.start()
-
+    g_s.over_x()
     for dl in range(2):
         for rel in (0, 1, 3, 2):
             wx[rel, dl].wait_recv()
-    mate = dev(z, xl, 1 - core, y, xh)
-    beside = dev(z, 1 - xl, core, y, xh)
-    kept, given = lanes256(xl), lanes256(1 - xl)
-
-    def l_dot(lo, n):
-        def product(d):
-            return jnp.dot(wt_all[d], l_all[d, :, pl.ds(lo, n)], preferred_element_type=F32)
-
-        return product
-
-    def s_dot(d):
-        return lax.dot_general(wt_all[d], wg[d], NT, preferred_element_type=F32)
-
-    class Group:
-        def __init__(self, i, part, send, got, xg, zg, product):
-            self.i, self.part, self.send, self.got, self.xg, self.zg = i, part, send, got, xg, zg
-            self.product = product
+    me_p = 4 * xl + z
+
+    class Straight:
+        def __init__(self, i, part, send, got, rs, product):
+            self.part, self.send, self.got, self.rs, self.product = part, send, got, rs, product
             self.pair = remote(send, got, cc_s.at[i], cc_r.at[i], mate)
-            self.side = remote(part.at[given, :], xg, xl_s.at[i], xl_r.at[i], beside)
-
-        def dots(self):
-            self.send[...] = self.product(1 - core)
-            self.pair.start()
-            self.part[...] = self.product(core)
-
-        def over_x(self):
+
+        dots = Group.dots
+
+        def copy(self, k):
+            dz, dx = OTHERS[k]
+            tz, tx = (z + dz) % 4, (xl + dx) % 2
+            return remote(self.part.at[part64(4 * tx + tz), :], self.rs.at[k], rf_s.at[k], rf_r.at[k],
+                          dev(tz, tx, core, y, xh))
+
+        def add(self):
             self.pair.wait_recv()
-            self.part[given, :] = self.part[given, :] + self.got[given, :]
-            self.side.start()
-            self.part[kept, :] = self.part[kept, :] + self.got[kept, :]
-
-        def line(self, k):
-            to = (z + k) % 4
-            return remote(self.xg.at[part64(to), :], self.zg.at[k - 1],
-                          zz_s.at[self.i, k - 1], zz_r.at[self.i, k - 1], dev(to, xl, core, y, xh))
-
-        def over_z(self):
-            self.side.wait_recv()
-            self.xg[...] = self.xg[...] + self.part[kept, :]
-            for k in (1, 3, 2):
-                self.line(k).start()
+            self.part[...] = self.part[...] + self.got[...]
+            for k in range(7):
+                self.copy(k).start()
 
         def total(self):
-            for k in (1, 3, 2):
-                self.line(k).wait_recv()
-            return (self.xg[part64(z), :] + self.zg[0]) + (self.zg[1] + self.zg[2])
+            for k in range(7):
+                self.copy(k).wait_recv()
+            total = self.part[part64(me_p), :]
+            for k in range(7):
+                total = total + self.rs[k]
+            return total
 
         def sent(self):
             self.pair.wait_send()
-            self.side.wait_send()
-            for k in (1, 3, 2):
-                self.line(k).wait_send()
+            for k in range(7):
+                self.copy(k).wait_send()
 
     me8 = 2 * z + xh
 
     def spread(u, k, block):
-        b = (me8 + k) % 8
-        return remote(red.at[u], e_all.at[part64(z), lanes128(block)], ag_s.at[u, k - 1], ag_r.at[u, k - 1],
-                      dev(b // 2, xl, core, y, b % 2))
+        dz, dx = OTHERS[k]
+        return remote(red.at[u], e_all.at[part64(z), lanes128(block)], ag_s.at[u, k], ag_r.at[u, k],
+                      dev((z + dz) % 4, xl, core, y, (xh + dx) % 2))
 
     def gather(value, u, rel):
         block = 2 * ((y + rel) % 4) + xh
         red[u] = value
-        loop(1, 8, lambda k: spread(u, k, block).start())
+        for k in range(7):
+            spread(u, k, block).start()
         e_all[part64(z), lanes128(block)] = value
 
+    def along(u, k, rel):
+        dz, _ = OTHERS[k]
+        pair = e_all.at[part64(z), lanes256((y + rel) % 4)]
+        return remote(pair, pair, ag_s.at[u, k], ag_r.at[u, k], dev((z + dz) % 4, xl, core, y, xh))
+
+    def gather_x(value, u, rel):
+        block = 2 * ((y + rel) % 4) + xh
+        red[u] = value
+        spread(u, 6, block).start()
+        e_all[part64(z), lanes128(block)] = value
+
+    def gather_z(u, rel):
+        spread(u, 6, 0).wait_recv()
+        for k in (3, 4, 5):
+            along(u, k, rel).start()
+
+    def gathered(u, rel):
+        for k in (3, 4, 5):
+            along(u, k, rel).wait_recv()
+
+    def gather_sent(u, rel):
+        for k in (3, 4, 5):
+            along(u, k, rel).wait_send()
+        spread(u, 6, 0).wait_send()
+
     g_o = Group(0, part_o, send_o, got_o, xg_o, zg_o, l_dot(0, 128))
-    g_f = Group(1, part_f, send_f, got_f, xg_f, zg_f, l_dot(128, 128))
-    g_s = Group(2, part_s, send_s, got_s, xg_s, zg_s, s_dot)
-
-    me_p = 4 * xl + z
-
-    def pair_n(dl):
-        return remote(two.at[dl], got_n, cc_s.at[3], cc_r.at[3], mate)
+    g_f = Straight(1, part_f, send_f, got_f, rs_f, l_dot(128, 128))
+    g_r = Specific(1, lanes256(1 - xh), differ, alike)
+
+
+    def pair_n(dl, h):
+        half = pl.ds(256 * h, 256)
+        return remote(two.at[dl, half, :], got_n.at[half, :], cc_s.at[3 + h], cc_r.at[3 + h], mate)
 
     def rn(k):
-        p = (me_p + k) % 8
-        return remote(two.at[core, part64(p), :], rs_n.at[k - 1], rn_s.at[k - 1], rn_r.at[k - 1],
-                      dev(p % 4, p // 4, core, y, xh))
+        dz, dx = OTHERS[k]
+        tz, tx = (z + dz) % 4, (xl + dx) % 2
+        return remote(two.at[core, part64(4 * tx + tz), :], rs_n.at[k], rn_s.at[k], rn_r.at[k],
+                      dev(tz, tx, core, y, xh))
 
     def near_dot(dl):
         for dy in near:
             ly[dy, dl].wait_recv()
-        two[dl] = jnp.dot(wt_all[dl], l_all[dl, :, pl.ds(256, 256)], preferred_element_type=F32)
-
-        @pl.when(core != dl)
-        def _():
-            pair_n(dl).start()
+        for h in range(2):
+            half = pl.ds(256 * h, 256)
+            two[dl, half, :] = jnp.dot(wt_all[dl, half, :], l_all[dl, :, pl.ds(256, 256)],
+                                       preferred_element_type=F32)
+
+            @pl.when(core != dl)
+            def _():
+                pair_n(dl, h).start()
 
     def near_add(dl):
         @pl.when(core == dl)
         def _():
-            pair_n(dl).wait_recv()
-            two[dl] = two[dl] + got_n[...]
-            loop(1, 8, lambda k: rn(k).start())
-
-    def near_gather(dl):
+            for h in range(2):
+                half = pl.ds(256 * h, 256)
+                pair_n(dl, h).wait_recv()
+                two[dl, half, :] = two[dl, half, :] + got_n[half, :]
+            for k in range(7):
+                rn(k).start()
+
+    def near_gather(dl, how):
         @pl.when(core == dl)
         def _():
-            loop(1, 8, lambda k: rn(k).wait_recv())
+            for k in range(7):
+                rn(k).wait_recv()
             total = two[dl, part64(me_p), :]
             for k in range(7):
                 total = total + rs_n[k]
-            gather(total[:, :128], 2, 1)
-            gather(total[:, 128:], 3, 3)
+            how(total[:, :128], 2, 1)
+            how(total[:, 128:], 3, 3)
 
     g_o.dots()
     g_o.over_x()
     near_dot(0)
-    g_s.dots()
+    g_r.dots()
     g_o.over_z()
     near_add(0)
-    g_s.over_x()
-    gather(g_o.total(), 0, 0)
+    g_r.over_z()
     for dl in range(2):
         ly[2, dl].wait_recv()
     g_f.dots()
-    g_f.over_x()
-    g_s.over_z()
-    near_gather(0)
-    g_f.over_z()
-    swap = remote(s_red, s_tile, sx_s, sx_r, dev(z, xh, core, y, xl))
-    s_red[...] = g_s.total()
-
-    @pl.when(xl != xh)
-    def _():
-        swap.start()
-
-    @pl.when(xl == xh)
-    def _():
-        s_tile[...] = s_red[...]
-
+    gather_x(g_o.total(), 0, 0)
+    g_f.add()
+    near_gather(0, gather_x)
+    gather_z(0, 0)
     for c in [*wy.values(), *wx.values(), *wf.values()]:
         c.wait_send()
+    g_r.over_x()
+
+    @pl.when(core == 0)
+    def _():
+        gather_z(2, 1)
+        gather_z(3, 3)
+
     gather(g_f.total(), 1, 2)
     near_dot(1)
+    @pl.when(turn == 0)
+    def _():
+        f_own.start()
+
+    @pl.when(turn != 0)
+    def _():
+        f_copy.start()
+
     near_add(1)
+    near_gather(1, gather)
 
     @pl.when(turn == 0)
     def _():
@@ -317,22 +447,34 @@
     def _():
         f_copy.wait_recv()
 
-    def left_part(u, rel):
-        loop(1, 8, lambda k: spread(u, k, 0).wait_recv())
+    def left_part(rel):
         at = lanes256((y + rel) % 4)
-        return lax.dot_general(e_all[:, at], f_rows[:, at], NT, precision=HIGH, preferred_element_type=F32)
-
-    left_val[...] = left_part(0, 0) + left_part(1, 2)
-    for g in (g_o, g_f, g_s):
-        g.sent()
-    near_gather(1)
-    left_val[...] += left_part(2, 1) + left_part(3, 3)
+        return dot_nt(e_all[:, at], f_rows[:, at])
+
+    gathered(0, 0)
+    for k in range(7):
+        spread(1, k, 0).wait_recv()
+    left_val[...] = left_part(0) + left_part(2)
+    g_o.sent()
+    g_f.sent()
+
+    @pl.when(core == 0)
+    def _():
+        gathered(2, 1)
+        gathered(3, 3)
+
+    @pl.when(core == 1)
+    def _():
+        for k in range(7):
+            spread(2, k, 0).wait_recv()
+            spread(3, k, 0).wait_recv()
+
+    left_val[...] += left_part(1) + left_part(3)
 
     def la(j):
         return remote(left_val.at[part64(j // 2), :], left_buf.at[:, lanes128(2 * yq + xh)],
                       la_s.at[j], la_r.at[me8], dev(j // 2, j % 2, core, y, xl))
 
-    alike = xl == xh
     me_t = 2 * z + xl
 
     def unless(skip, body):
@@ -346,15 +488,42 @@
     def _():
         left_buf[:, lanes128(2 * yq + xh)] = left_val[part64(z), :]
 
-    for u in range(4):
-        loop(1, 8, lambda k, u=u: spread(u, k, 0).wait_send())
-    loop(1, 8, lambda k: rn(k).wait_send())
+    swap = remote(s_red, s_tile, sx_s, sx_r, dev(z, xh, core, y, xl))
+
+    @pl.when(alike)
+    def _():
+        s_tile[...] = g_s.total()
+
+    @pl.when(differ)
+    def _():
+        s_red[...] = g_r.total()
+        swap.start()
+
+    g_s.sent()
+    g_r.sent()
+    gather_sent(0, 0)
+    for k in range(7):
+        spread(1, k, 0).wait_send()
+
+    @pl.when(core == 0)
+    def _():
+        gather_sent(2, 1)
+        gather_sent(3, 3)
+
+    @pl.when(core == 1)
+    def _():
+        for k in range(7):
+            spread(2, k, 0).wait_send()
+            spread(3, k, 0).wait_send()
+
+    for k in range(7):
+        rn(k).wait_send()
 
     def la_in(j):
         return remote(left_val.at[part64(0), :], left_buf.at[:, lanes128(0)], la_s.at[0], la_r.at[j], mate)
 
     loop(0, 8, lambda j: unless(jnp.logical_and(alike, j == me8), lambda: la_in(j).wait_recv()))
-    tile = lax.dot_general(left_buf[...], e_all[...], NT, precision=HIGH, preferred_element_type=F32)
+    tile = dot_nt(left_buf[...], e_all[...])
 
     @pl.when(xl != xh)
     def _():
@@ -377,7 +546,8 @@
 
     for c in [*ly.values(), *lf.values()]:
         c.wait_send()
-    pair_n(1 - core).wait_send()
+    for h in range(2):
+        pair_n(1 - core, h).wait_send()
 
     @pl.when(xl != xh)
     def _():
@@ -403,7 +573,6 @@
     any_ = pl.BlockSpec(memory_space=pl.ANY)
     vmem = pl.BlockSpec(memory_space=pltpu.VMEM)
     dma = pltpu.SemaphoreType.DMA
-    widths = (128, 128, 256)
     return pl.pallas_call(
         kernel,
         out_shape=jax.ShapeDtypeStruct((8, 32, 64), F32),
@@ -416,11 +585,15 @@
             pltpu.VMEM((2, assets, 128), BF16),
             pltpu.VMEM((2, 256, assets), BF16),
             pltpu.VMEM((128, 1024), F32),
-            *[pltpu.VMEM((512, w), F32) for w in widths],
-            *[pltpu.VMEM((512, w), F32) for w in widths],
-            *[pltpu.VMEM((512, w), F32) for w in widths],
-            *[pltpu.VMEM((256, w), F32) for w in widths],
-            *[pltpu.VMEM((3, 64, w), F32) for w in widths],
+            *[pltpu.VMEM((512, 128), F32)] * 3,
+            pltpu.VMEM((256, 128), F32),
+            pltpu.VMEM((3, 64, 128), F32),
+            *[pltpu.VMEM((512, 128), F32)] * 3,
+            pltpu.VMEM((7, 64, 128), F32),
+            *[pltpu.VMEM((2, 256, 256), F32)] * 3,
+            pltpu.VMEM((2, 3, 64, 256), F32),
+            pltpu.VMEM((2, 64, 256), F32),
+            pltpu.VMEM((2, 64, 256), F32),
             pltpu.VMEM((2, 512, 256), F32),
             pltpu.VMEM((512, 256), F32),
             pltpu.VMEM((7, 64, 256), F32),
@@ -434,8 +607,9 @@
             pltpu.VMEM((8, 32, 64), F32),
             dma((3, 2)), dma((3, 2)), dma((3, 2)), dma((3, 2)), dma((4, 2)), dma((4, 2)),
             dma((2,)), dma((2,)), dma((2,)), dma((2,)), dma((5,)), dma, dma,
-            dma((4,)), dma((4,)), dma((3,)), dma((3,)), dma((3, 3)), dma((3, 3)), dma((7,)), dma((7,)),
-            dma((4, 7)), dma((4, 7)), dma, dma, dma((8,)), dma((8,)), dma((8,)), dma((8,)),
+            dma((5,)), dma((5,)), dma((3,)), dma((3,)), dma((3, 3)), dma((3, 3)), dma((7,)), dma((7,)), dma((7,)), dma((7,)),
+            dma((4, 7)), dma((4, 7)), dma, dma,
+            dma((2,)), dma((2,)), dma((2, 3)), dma((2, 3)), dma((2,)), dma((2,)), dma((8,)), dma((8,)), dma((8,)), dma((8,)),
         ],
         compiler_params=pltpu.CompilerParams(collective_id=0, has_side_effects=True),
     )(loadings, wt, specific, factor_cov)

time: 117 us -> 108 us (0.923)
  Pallas kernels: 115 us -> 107 us
    pallas_call x1, Pallas kernels: 115 us -> 107 us  [shards(): pl.pallas_call(kernel, out_shape=jax.ShapeDtypeStruct((8, 32, 64), F32),...]
where the time goes in v3:
time: 108 us
  Pallas kernels  107 us (99%)
  local copies, waits for them, and re-layouts  1.57 us (1%)
    pallas_call x1, Pallas kernels, shards(): pl.pallas_call(kernel, out_shape=jax.ShapeDtypeStruct((8, 32, 64), F32),...  107 us

profile of v3, /device:TPU:1, one launch (start us, length us, event | category | flops | bytes accessed | tf_op | source)
XLA Modules:
  0.0 108.2 jit_solution(5218580249564020571)
XLA Ops:
  0.0 106.7 %shard_map.46 = f32[8,32,64]{2,1,0:T(8,128)} custom-call(bf16[8,2048,128]{2,1,0:T(8,128)(2,1)} %load_ref.1, bf16[8,64,2048]{2,1,0:T(8,128)(2,1)} %bitcast.1, f32[8,2048]{1,0:T(8,128)} %spec_ref.1, f32[8,128,1024]{2,1,0:T(8,128)} %fcov_ref.1), custom_call_target="tpu_custom_call" | custom-call | tf_op jit(solution)/shard_map/pallas_call | solution.py:576
  106.7 1.6 %copy.6 = f32[8,32,64]{2,1,0:T(8,128)} copy(f32[8,32,64]{2,1,0:T(8,128)} %shard_map.46) | data formatting | bytes 131072

commit v4 on v3

--- a/solution.py
+++ b/solution.py
@@ -28,10 +28,10 @@
 
 
 def kernel(load_ref, wt_ref, spec_ref, fcov_ref, out_ref,
-           wt_all, l_all, w_pass, l_pass, wg, f_rows,
+           wt_all, l_all, w_pass, l_pass, spec, wg, f_rows,
            part_o, send_o, got_o, xg_o, zg_o, part_f, send_f, got_f, rs_f,
            part_s, send_s, got_s, zg_s, sum_s, in_s,
-           two, got_n, rs_n, red, s_red, s_tile, e_all, left_val, left_buf, obuf, oin,
+           two, got_n, rs_n, red, s_red, s_tile, e_all, left_val, left_buf, obuf,
            wy_s, wy_r, ly_s, ly_r, wx_s, wx_r, wf_s, wf_r, lf_s, lf_r, loc, f_s, f_r,
            cc_s, cc_r, xl_s, xl_r, zz_s, zz_r, rf_s, rf_r, rn_s, rn_r, ag_s, ag_r, sx_s, sx_r, sd_s, sd_r, sl_s, sl_r, sc_s, sc_r,
            la_s, la_r, fo_s, fo_r):
@@ -69,28 +69,14 @@
     def greet(to):
         pl.semaphore_signal(bar, inc=1, device_id=to, device_id_type=MESH)
 
-    def greet_line(k):
-        a = (core * 4 + y + k) % 8
-        greet(dev(z, xl, a // 4, a % 4, xh))
-
-    def greet_plane(k):
-        b = (z * 4 + xl * 2 + xh + k) % 16
-        greet(dev(b // 4, (b // 2) % 2, core, y, b % 2))
-
-    def greet_swap(k):
-        greet(dev(z, xh, k // 4, k % 4, xl))
-
-    loop(1, 8, greet_line)
-    loop(1, 16, greet_plane)
-
-    @pl.when(xl != xh)
-    def _():
-        loop(0, 8, greet_swap)
-        pl.semaphore_wait(bar, 30)
-
-    @pl.when(xl == xh)
-    def _():
-        pl.semaphore_wait(bar, 22)
+    for k in (1, 2, 3):
+        greet(dev((z + k) % 4, xl, core, y, xh))
+    for k in (1, 3):
+        greet(dev(z, xl, core, (y + k) % 4, xh))
+    greet(dev(z, 1 - xl, core, y, xh))
+    greet(dev(z, xl, core, y, 1 - xh))
+    greet(dev(z, xl, 1 - core, y, xh))
+    pl.semaphore_wait(bar, 8)
 
     def block_of(b):
         return part64(4 * xh + b)
@@ -138,6 +124,8 @@
     for dl in range(2):
         own.append(pltpu.make_async_copy(load_ref.at[2 * y + dl], l_all.at[dl, :, pl.ds(0, 128)], loc.at[2 + dl]))
         own[-1].start()
+    own.append(pltpu.make_async_copy(spec_ref, spec, loc.at[5]))
+    own[-1].start()
     w_arrived(1, 0)
     w_arrived(3, 0)
     for dl in range(2):
@@ -158,7 +146,7 @@
     for c in own:
         c.wait()
     for dl in range(2):
-        scale = spec_ref[pl.ds(2 * y + dl, 1), :]
+        scale = spec[pl.ds(2 * y + dl, 1), :]
         w = wt_all[dl, lanes256(xh), :]
         wg[dl] = (scale * w.astype(F32)).astype(BF16)
     mate = dev(z, xl, 1 - core, y, xh)
@@ -361,7 +349,7 @@
 
 
     def pair_n(dl, h):
-        half = pl.ds(256 * h, 256)
+        half = (given, kept)[h]
         return remote(two.at[dl, half, :], got_n.at[half, :], cc_s.at[3 + h], cc_r.at[3 + h], mate)
 
     def rn(k):
@@ -373,8 +361,7 @@
     def near_dot(dl):
         for dy in near:
             ly[dy, dl].wait_recv()
-        for h in range(2):
-            half = pl.ds(256 * h, 256)
+        for h, half in enumerate((given, kept)):
             two[dl, half, :] = jnp.dot(wt_all[dl, half, :], l_all[dl, :, pl.ds(256, 256)],
                                        preferred_element_type=F32)
 
@@ -385,12 +372,12 @@
     def near_add(dl):
         @pl.when(core == dl)
         def _():
-            for h in range(2):
-                half = pl.ds(256 * h, 256)
+            for h, half in enumerate((given, kept)):
                 pair_n(dl, h).wait_recv()
                 two[dl, half, :] = two[dl, half, :] + got_n[half, :]
-            for k in range(7):
-                rn(k).start()
+                for k in range(7):
+                    if OTHERS[k][1] == 1 - h:
+                        rn(k).start()
 
     def near_gather(dl, how):
         @pl.when(core == dl)
@@ -535,14 +522,15 @@
             obuf[4 * h + b] = tile[32 * h:32 * h + 32, 64 * b:64 * b + 64]
 
     def fo(i):
-        return remote(obuf.at[i], oin.at[day], fo_s.at[i], fo_r.at[day], dev(z, xh, i // 4, i % 4, xl))
+        return remote(obuf.at[i], out_ref.at[day], fo_s.at[i], fo_r.at[day], dev(z, xh, i // 4, i % 4, xl))
 
     me_o = 4 * core + y
+    stay = pltpu.make_async_copy(obuf.at[me_o], out_ref.at[day], loc.at[6])
     loop(0, 8, lambda i: unless(jnp.logical_and(alike, i == me_o), lambda: fo(i).start()))
 
     @pl.when(alike)
     def _():
-        oin[day] = obuf[me_o]
+        stay.start()
 
     for c in [*ly.values(), *lf.values()]:
         c.wait_send()
@@ -560,10 +548,14 @@
     loop(0, 8, lambda j: unless(jnp.logical_and(alike, j == me_t), lambda: la(j).wait_send()))
 
     def fo_in(d):
-        return remote(obuf.at[0], oin.at[d], fo_s.at[0], fo_r.at[d], mate)
+        return remote(obuf.at[0], out_ref.at[d], fo_s.at[0], fo_r.at[d], mate)
 
     loop(0, 8, lambda d: unless(jnp.logical_and(alike, d == day), lambda: fo_in(d).wait_recv()))
-    out_ref[...] = oin[...]
+
+    @pl.when(alike)
+    def _():
+        stay.wait()
+
     loop(0, 8, lambda i: unless(jnp.logical_and(alike, i == me_o), lambda: fo(i).wait_send()))
 
 
@@ -571,18 +563,18 @@
     assets = loadings.shape[1]
     wt = jnp.swapaxes(weights, 1, 2)
     any_ = pl.BlockSpec(memory_space=pl.ANY)
-    vmem = pl.BlockSpec(memory_space=pltpu.VMEM)
     dma = pltpu.SemaphoreType.DMA
     return pl.pallas_call(
         kernel,
         out_shape=jax.ShapeDtypeStruct((8, 32, 64), F32),
-        in_specs=[any_, any_, vmem, any_],
-        out_specs=vmem,
+        in_specs=[any_] * 4,
+        out_specs=any_,
         scratch_shapes=[
             pltpu.VMEM((2, 512, assets), BF16),
             pltpu.VMEM((2, assets, 512), BF16),
             pltpu.VMEM((2, 64, assets), BF16),
             pltpu.VMEM((2, assets, 128), BF16),
+            pltpu.VMEM((8, assets), F32),
             pltpu.VMEM((2, 256, assets), BF16),
             pltpu.VMEM((128, 1024), F32),
             *[pltpu.VMEM((512, 128), F32)] * 3,
@@ -604,9 +596,8 @@
             pltpu.VMEM((256, 128), F32),
             pltpu.VMEM((64, 1024), F32),
             pltpu.VMEM((8, 32, 64), F32),
-            pltpu.VMEM((8, 32, 64), F32),
             dma((3, 2)), dma((3, 2)), dma((3, 2)), dma((3, 2)), dma((4, 2)), dma((4, 2)),
-            dma((2,)), dma((2,)), dma((2,)), dma((2,)), dma((5,)), dma, dma,
+            dma((2,)), dma((2,)), dma((2,)), dma((2,)), dma((7,)), dma, dma,
             dma((5,)), dma((5,)), dma((3,)), dma((3,)), dma((3, 3)), dma((3, 3)), dma((7,)), dma((7,)), dma((7,)), dma((7,)),
             dma((4, 7)), dma((4, 7)), dma, dma,
             dma((2,)), dma((2,)), dma((2, 3)), dma((2, 3)), dma((2,)), dma((2,)), dma((8,)), dma((8,)), dma((8,)), dma((8,)),

time: 108 us -> 106 us (0.981)
  Pallas kernels: 107 us -> 104 us
    pallas_call x1, Pallas kernels: 107 us -> 104 us  [shards(): pl.pallas_call(kernel, out_shape=jax.ShapeDtypeStruct((8, 32, 64), F32),...]
where the time goes in v4:
time: 106 us
  Pallas kernels  104 us (98%)
  local copies, waits for them, and re-layouts  1.57 us (1%)
    pallas_call x1, Pallas kernels, shards(): pl.pallas_call(kernel, out_shape=jax.ShapeDtypeStruct((8, 32, 64), F32),...  104 us

profile of v4, /device:TPU:1, one launch (start us, length us, event | category | flops | bytes accessed | tf_op | source)
XLA Modules:
  0.0 105.6 jit_solution(14827723313258884881)
XLA Ops:
  0.0 104.0 %shard_map.46 = f32[8,32,64]{2,1,0:T(8,128)} custom-call(bf16[8,2048,128]{2,1,0:T(8,128)(2,1)} %load_ref.1, bf16[8,64,2048]{2,1,0:T(8,128)(2,1)} %bitcast.1, f32[8,2048]{1,0:T(8,128)} %spec_ref.1, f32[8,128,1024]{2,1,0:T(8,128)} %fcov_ref.1), custom_call_target="tpu_custom_call" | custom-call | tf_op jit(solution)/shard_map/pallas_call | solution.py:567
  104.0 1.6 %copy.6 = f32[8,32,64]{2,1,0:T(8,128)} copy(f32[8,32,64]{2,1,0:T(8,128)} %shard_map.46) | data formatting | bytes 131072

commit v5 on v4

--- a/solution.py
+++ b/solution.py
@@ -84,6 +84,8 @@
     here = block_of(y)
     across = dev(z, xl, core, y, 1 - xh)
     near = (1, 3)
+    assets = l_all.shape[1]
+    most, rest = pl.ds(0, 3 * assets // 4), pl.ds(3 * assets // 4, assets // 4)
     own = []
     wy, wx, ly, wf, lf = {}, {}, {}, {}, {}
 
@@ -105,9 +107,17 @@
 
     def l_near(dy, dl):
         ty = (y + dy) % 4
-        ly[dy, dl] = remote(load_ref.at[2 * ty + dl], l_all.at[dl, :, pl.ds(128 * SLOT[4 - dy], 128)],
-                            ly_s.at[dy - 1, dl], ly_r.at[dy - 1, dl], dev(z, xl, core, ty, xh))
-        ly[dy, dl].start()
+        slot = pl.ds(128 * SLOT[4 - dy], 128)
+        to = dev(z, xl, core, ty, xh)
+        if dl == 0:
+            ly[dy, dl] = remote(load_ref.at[2 * ty], l_all.at[0, :, slot],
+                                ly_s.at[dy - 1, 0], ly_r.at[dy - 1, 0], to)
+            ly[dy, dl].start()
+            return
+        for rows, i in ((most, 1), (rest, 2)):
+            ly[dy, i] = remote(load_ref.at[2 * ty + 1, rows, :], l_all.at[1, rows, slot],
+                               ly_s.at[dy - 1, i], ly_r.at[dy - 1, i], to)
+            ly[dy, i].start()
 
     for dy in near:
         w_near(dy, 0)
@@ -311,23 +321,27 @@
         return remote(red.at[u], e_all.at[part64(z), lanes128(block)], ag_s.at[u, k], ag_r.at[u, k],
                       dev((z + dz) % 4, xl, core, y, (xh + dx) % 2))
 
-    def gather(value, u, rel):
-        block = 2 * ((y + rel) % 4) + xh
-        red[u] = value
+    def gather(items):
+        blocks = [2 * ((y + rel) % 4) + xh for _, _, rel in items]
+        for value, u, _ in items:
+            red[u] = value
         for k in range(7):
-            spread(u, k, block).start()
-        e_all[part64(z), lanes128(block)] = value
+            for (_, u, _), block in zip(items, blocks):
+                spread(u, k, block).start()
+        for (value, _, _), block in zip(items, blocks):
+            e_all[part64(z), lanes128(block)] = value
 
     def along(u, k, rel):
         dz, _ = OTHERS[k]
         pair = e_all.at[part64(z), lanes256((y + rel) % 4)]
         return remote(pair, pair, ag_s.at[u, k], ag_r.at[u, k], dev((z + dz) % 4, xl, core, y, xh))
 
-    def gather_x(value, u, rel):
-        block = 2 * ((y + rel) % 4) + xh
-        red[u] = value
-        spread(u, 6, block).start()
-        e_all[part64(z), lanes128(block)] = value
+    def gather_x(items):
+        for value, u, rel in items:
+            block = 2 * ((y + rel) % 4) + xh
+            red[u] = value
+            spread(u, 6, block).start()
+            e_all[part64(z), lanes128(block)] = value
 
     def gather_z(u, rel):
         spread(u, 6, 0).wait_recv()
@@ -358,12 +372,21 @@
         return remote(two.at[core, part64(4 * tx + tz), :], rs_n.at[k], rn_s.at[k], rn_r.at[k],
                       dev(tz, tx, core, y, xh))
 
+    def piece(dl, half, rows):
+        return jnp.dot(wt_all[dl, half, rows], l_all[dl, rows, pl.ds(256, 256)], preferred_element_type=F32)
+
     def near_dot(dl):
-        for dy in near:
-            ly[dy, dl].wait_recv()
+        if dl == 0:
+            for dy in near:
+                ly[dy, 0].wait_recv()
+        else:
+            for dy in near:
+                ly[dy, 2].wait_recv()
         for h, half in enumerate((given, kept)):
-            two[dl, half, :] = jnp.dot(wt_all[dl, half, :], l_all[dl, :, pl.ds(256, 256)],
-                                       preferred_element_type=F32)
+            if dl == 0:
+                two[dl, half, :] = piece(dl, half, slice(None))
+            else:
+                two[dl, half, :] = two[dl, half, :] + piece(dl, half, rest)
 
             @pl.when(core != dl)
             def _():
@@ -387,8 +410,7 @@
             total = two[dl, part64(me_p), :]
             for k in range(7):
                 total = total + rs_n[k]
-            how(total[:, :128], 2, 1)
-            how(total[:, 128:], 3, 3)
+            how(((total[:, :128], 2, 1), (total[:, 128:], 3, 3)))
 
     g_o.dots()
     g_o.over_x()
@@ -400,20 +422,22 @@
     for dl in range(2):
         ly[2, dl].wait_recv()
     g_f.dots()
-    gather_x(g_o.total(), 0, 0)
+    gather_x(((g_o.total(), 0, 0),))
     g_f.add()
     near_gather(0, gather_x)
     gather_z(0, 0)
     for c in [*wy.values(), *wx.values(), *wf.values()]:
         c.wait_send()
-    g_r.over_x()
+    for dy in near:
+        ly[dy, 1].wait_recv()
+    two[1] = piece(1, slice(None), most)
 
     @pl.when(core == 0)
     def _():
         gather_z(2, 1)
         gather_z(3, 3)
 
-    gather(g_f.total(), 1, 2)
+    gather(((g_f.total(), 1, 2),))
     near_dot(1)
     @pl.when(turn == 0)
     def _():
@@ -424,6 +448,7 @@
         f_copy.start()
 
     near_add(1)
+    g_r.over_x()
     near_gather(1, gather)
 
     @pl.when(turn == 0)
@@ -596,7 +621,7 @@
             pltpu.VMEM((256, 128), F32),
             pltpu.VMEM((64, 1024), F32),
             pltpu.VMEM((8, 32, 64), F32),
-            dma((3, 2)), dma((3, 2)), dma((3, 2)), dma((3, 2)), dma((4, 2)), dma((4, 2)),
+            dma((3, 2)), dma((3, 2)), dma((3, 3)), dma((3, 3)), dma((4, 2)), dma((4, 2)),
             dma((2,)), dma((2,)), dma((2,)), dma((2,)), dma((7,)), dma, dma,
             dma((5,)), dma((5,)), dma((3,)), dma((3,)), dma((3, 3)), dma((3, 3)), dma((7,)), dma((7,)), dma((7,)), dma((7,)),
             dma((4, 7)), dma((4, 7)), dma, dma,

time: 106 us -> 105 us (level)
  no operation moved by 1% of the time
where the time goes in v5:
time: 105 us
  Pallas kernels  103 us (98%)
  local copies, waits for them, and re-layouts  1.57 us (1%)
    pallas_call x1, Pallas kernels, shards(): pl.pallas_call(kernel, out_shape=jax.ShapeDtypeStruct((8, 32, 64), F32),...  103 us

profile of v5, /device:TPU:1, one launch (start us, length us, event | category | flops | bytes accessed | tf_op | source)
XLA Modules:
  0.0 104.8 jit_solution(1270048889495675646)
XLA Ops:
  0.0 103.2 %shard_map.46 = f32[8,32,64]{2,1,0:T(8,128)} custom-call(bf16[8,2048,128]{2,1,0:T(8,128)(2,1)} %load_ref.1, bf16[8,64,2048]{2,1,0:T(8,128)(2,1)} %bitcast.1, f32[8,2048]{1,0:T(8,128)} %spec_ref.1, f32[8,128,1024]{2,1,0:T(8,128)} %fcov_ref.1), custom_call_target="tpu_custom_call" | custom-call | tf_op jit(solution)/shard_map/pallas_call | solution.py:592
  103.2 1.6 %copy.6 = f32[8,32,64]{2,1,0:T(8,128)} copy(f32[8,32,64]{2,1,0:T(8,128)} %shard_map.46) | data formatting | bytes 131072

commit v6 on v5

--- a/solution.py
+++ b/solution.py
@@ -535,23 +535,24 @@
         return remote(left_val.at[part64(0), :], left_buf.at[:, lanes128(0)], la_s.at[0], la_r.at[j], mate)
 
     loop(0, 8, lambda j: unless(jnp.logical_and(alike, j == me8), lambda: la_in(j).wait_recv()))
-    tile = dot_nt(left_buf[...], e_all[...])
-
-    @pl.when(xl != xh)
+
+    @pl.when(differ)
     def _():
         swap.wait_recv()
-
-    tile = tile + s_tile[...]
-    for h in range(2):
-        for b in range(4):
-            obuf[4 * h + b] = tile[32 * h:32 * h + 32, 64 * b:64 * b + 64]
 
     def fo(i):
         return remote(obuf.at[i], out_ref.at[day], fo_s.at[i], fo_r.at[day], dev(z, xh, i // 4, i % 4, xl))
 
     me_o = 4 * core + y
     stay = pltpu.make_async_copy(obuf.at[me_o], out_ref.at[day], loc.at[6])
-    loop(0, 8, lambda i: unless(jnp.logical_and(alike, i == me_o), lambda: fo(i).start()))
+    for c in range(2):
+        cols = slice(128 * c, 128 * c + 128)
+        tile = dot_nt(left_buf[...], e_all[cols, :]) + s_tile[:, cols]
+        for h in range(2):
+            for b in range(2):
+                i = 4 * h + 2 * c + b
+                obuf[i] = tile[32 * h:32 * h + 32, 64 * b:64 * b + 64]
+                unless(jnp.logical_and(alike, i == me_o), lambda: fo(i).start())
 
     @pl.when(alike)
     def _():

time: 105 us -> 105 us (level)
  no operation moved by 1% of the time
where the time goes in v6:
time: 105 us; the launch traced here: 104 us
  Pallas kernels  103 us (98%)
  local copies, waits for them, and re-layouts  1.57 us (1%)
    pallas_call x1, Pallas kernels, shards(): pl.pallas_call(kernel, out_shape=jax.ShapeDtypeStruct((8, 32, 64), F32),...  103 us

profile of v6, /device:TPU:1, one launch (start us, length us, event | category | flops | bytes accessed | tf_op | source)
XLA Modules:
  0.0 104.4 jit_solution(13652194440810402757)
XLA Ops:
  0.0 102.8 %shard_map.46 = f32[8,32,64]{2,1,0:T(8,128)} custom-call(bf16[8,2048,128]{2,1,0:T(8,128)(2,1)} %load_ref.1, bf16[8,64,2048]{2,1,0:T(8,128)(2,1)} %bitcast.1, f32[8,2048]{1,0:T(8,128)} %spec_ref.1, f32[8,128,1024]{2,1,0:T(8,128)} %fcov_ref.1), custom_call_target="tpu_custom_call" | custom-call | tf_op jit(solution)/shard_map/pallas_call | solution.py:593
  102.8 1.6 %copy.6 = f32[8,32,64]{2,1,0:T(8,128)} copy(f32[8,32,64]{2,1,0:T(8,128)} %shard_map.46) | data formatting | bytes 131072
